TPU v7x, 32 devices: a whole 2x2x4 slice. The times are simulated.
32 devices in a mesh: kpt: 2 (over y), row: 4 (over x, core), col: 4 (over z).
Axes of the slice: x: 2, y: 2, z: 4, core: 2. Of those that a mesh axis runs over, the one named last changes fastest.
Arguments:
- left_blocks: bfloat16 [8, 64, 2, 2, 128, 128], P(('kpt', 'row'), 'col'), parts along dimension 0, may hold values from -0.5 to 0.5
- left_rows: int32 [8, 64, 2], P(('kpt', 'row'), 'col'), parts along dimension 0, may hold values from 0 to 7, as said below
- left_count: int32 [8, 64], P(('kpt', 'row'), 'col'), parts along dimension 0, may hold values from 1 to 2, as said below
- left_level: int32 [8, 64, 2], P(('kpt', 'row'), 'col'), parts along dimension 0, may hold values from 0 to 7
- right_blocks: bfloat16 [2, 64, 4, 4, 2, 128, 128], P('kpt', 'row', 'col'), parts along dimension 0, may hold values from -6 to 6
- right_cols: int32 [2, 64, 4, 4], P('kpt', 'row', 'col'), parts along dimension 0, may hold values from 0 to 15, as said below
- right_count: int32 [2, 64, 4], P('kpt', 'row', 'col'), parts along dimension 0, may hold values from 1 to 4, as said below
- right_level: int32 [2, 64, 4, 4], P('kpt', 'row', 'col'), parts along dimension 0, may hold values from 0 to 7
Outputs:
- product_blocks: bfloat16 [64, 64, 2, 128, 128], P(('kpt', 'row'), 'col'), parts along dimension 0
There are 2 independent parts, one for each index of `kpt`. A program takes and returns all parts, laid end to end along the dimension named above; each array names one. Nothing has to cross between parts.
Inputs may be any that keep to these rules, and one draw needn't show every extreme that they name: `left_rows`: the 2 slots of one row group and block column name distinct block rows. `left_count`: in every row group some block column has all 2 slots live. `right_cols`: the 4 slots of one block row and column group name distinct block columns. `right_count`: in every column group some block row has all 4 slots live.
All inputs are finite; a program needn't handle non-finite values.
Results may differ from a plain program's by a relative error of at most 0.001.
Values may be sent and summed in bfloat16 or wider, within the bound.
A program may use at most 256 MiB of HBM per device.

v0:
```python
import jax
import jax.numpy as jnp
from jax import lax
from jax.sharding import PartitionSpec as P

GR = 8
LEVEL_CUT = 7


def pair_products(left_pack, right_pack, total):
    left_blocks, left_rows, left_count, left_level = left_pack
    right_blocks, right_cols, right_count, right_level = right_pack
    slots_left = left_rows.shape[1]
    slots_right = right_cols.shape[1]
    live_left = jnp.arange(slots_left, dtype=jnp.int32)[None, :] < left_count[:, None]
    live_right = jnp.arange(slots_right, dtype=jnp.int32)[None, :] < right_count[:, None]
    kept = live_left[:, :, None] & live_right[:, None, :]
    kept = kept & (left_level[:, :, None] + right_level[:, None, :] >= LEVEL_CUT)
    terms = jnp.einsum(
        "kmcij,kndjl->kmncdil", left_blocks, right_blocks, preferred_element_type=jnp.float32
    )
    real_part = terms[:, :, :, 0, 0] - terms[:, :, :, 1, 1]
    imag_part = terms[:, :, :, 0, 1] + terms[:, :, :, 1, 0]
    product = jnp.stack([real_part, imag_part], axis=3) * kept[:, :, :, None, None, None].astype(
        jnp.float32
    )
    row_index = jnp.broadcast_to(left_rows[:, :, None], kept.shape).reshape(-1)
    col_index = jnp.broadcast_to(right_cols[:, None, :], kept.shape).reshape(-1)
    width = left_blocks.shape[-1]
    return total.at[row_index, col_index].add(product.reshape(-1, 2, width, width))


def body(
    left_blocks,
    left_rows,
    left_count,
    left_level,
    right_blocks,
    right_cols,
    right_count,
    right_level,
):
    left_pack = (left_blocks[0], left_rows[0], left_count[0], left_level[0])
    right_pack = (
        right_blocks[:, :, 0],
        right_cols[:, :, 0],
        right_count[:, :, 0],
        right_level[:, :, 0],
    )
    width = left_blocks.shape[-1]
    panel_rows = left_blocks.shape[1]
    total = jnp.zeros((GR, panel_rows, 2, width, width), jnp.float32)
    whole = (
        lax.all_gather(right_pack[0], "row", axis=1, tiled=True),
        lax.all_gather(right_pack[1], "row", axis=1, tiled=True),
        lax.all_gather(right_pack[2], "row", axis=1, tiled=True),
        lax.all_gather(right_pack[3], "row", axis=1, tiled=True),
    )
    merged = whole[0].shape[0] * whole[0].shape[1]
    flat = jax.tree.map(lambda member: member.reshape((merged,) + member.shape[2:]), whole)
    carry = total
    piece = (
        lax.all_gather(left_pack[0], "col", axis=0, tiled=True),
        lax.all_gather(left_pack[1], "col", axis=0, tiled=True),
        lax.all_gather(left_pack[2], "col", axis=0, tiled=True),
        lax.all_gather(left_pack[3], "col", axis=0, tiled=True),
    )
    count = piece[0].shape[0]
    for first in range(0, count, panel_rows):
        size = min(panel_rows, count - first)
        left_part = jax.tree.map(lambda member: member[first : first + size], piece)
        right_part = jax.tree.map(
            lambda member: lax.dynamic_slice_in_dim(member, first, size, 0), flat
        )
        carry = pair_products(left_part, right_part, carry)
    total = carry
    return total.astype(jnp.bfloat16)


def solution(mesh):
    in_specs = (
        P(("kpt", "row"), "col", None, None, None, None),
        P(("kpt", "row"), "col", None),
        P(("kpt", "row"), "col"),
        P(("kpt", "row"), "col", None),
        P("kpt", "row", "col", None, None, None, None),
        P("kpt", "row", "col", None),
        P("kpt", "row", "col"),
        P("kpt", "row", "col", None),
    )
    out_specs = P(("kpt", "row"), "col", None, None, None)
    return jax.shard_map(body, mesh=mesh, in_specs=in_specs, out_specs=out_specs, check_vma=False)
```

profile of v0, /device:TPU:1, one launch (start us, length us, event | category | flops | bytes accessed | tf_op | source)
XLA Modules:
  0.0 728.5 jit_solution(17531730856529968428)
XLA Ops:
  6.5 0.7 all-gather.11.cloned.1.call-update
  8.0 1.2 dynamic-slice.1
  9.3 1.2 dynamic-slice
  11.7 0.8 copy.67
  12.4 0.8 copy.70
  13.2 11.6 %all-gather.6 = s32[1,64,2]{2,0,1:T(1,128)S(1)} all-gather(s32[1,16,2]{2,0,1:T(1,128)S(1)} %copy.67), channel_id=8, replica_groups=mesh['kpt'=2,'row'=4,'col'=4] {'col'}, dimensions={1}, use_global_device_ids=true | all-gather | bytes 640 | tf_op jit(solution)/shard_map/all_gather | solution.py:66
  24.8 0.7 bitcast_dynamic-update-slice_fusion
  25.5 7.5 %all-reduce.1 = s32[64]{0:T(128)S(1)} all-reduce(s32[64]{0:T(128)S(1)} %bitcast_dynamic-update-slice_fusion), channel_id=7, replica_groups=mesh['kpt'=2,'row'=4,'col'=4] {'row'}, use_global_device_ids=true, to_apply=%add.1 | all-reduce | flops 64 | bytes 512
  33.0 0.7 bitcast_dynamic-update-slice_fusion.1
  33.7 6.5 all-reduce
  40.2 7.5 %all-gather.7 = s32[1,64,1,4]{3,2,0,1:T(1,128)S(1)} all-gather(s32[1,16,1,4]{3,2,0,1:T(1,128)S(1)} %copy.70), channel_id=9, replica_groups=mesh['kpt'=2,'row'=4,'col'=4] {'row'}, dimensions={1}, use_global_device_ids=true | all-gather | bytes 1280 | tf_op jit(solution)/shard_map/all_gather | solution.py:57
  48.3 0.8 copy.55
  49.0 10.2 %all-gather = s32[1,64,2]{2,0,1:T(1,128)S(1)} all-gather(s32[1,16,2]{2,0,1:T(1,128)S(1)} %copy.55), channel_id=2, replica_groups=mesh['kpt'=2,'row'=4,'col'=4] {'col'}, dimensions={1}, use_global_device_ids=true | all-gather | bytes 640 | tf_op jit(solution)/shard_map/all_gather | solution.py:64
  59.5 0.8 copy.58
  60.2 8.3 %all-gather.1 = s32[1,64,1,4]{3,2,0,1:T(1,128)S(1)} all-gather(s32[1,16,1,4]{3,2,0,1:T(1,128)S(1)} %copy.58), channel_id=3, replica_groups=mesh['kpt'=2,'row'=4,'col'=4] {'row'}, dimensions={1}, use_global_device_ids=true | all-gather | bytes 1280 | tf_op jit(solution)/shard_map/all_gather | solution.py:55
  73.9 43.8 %all-gather.11.cloned.1.call-done = bf16[1,64,1,4,2,128,128]{6,5,4,3,2,0,1:T(8,128)(2,1)} async-done(((bf16[1,16,1,4,2,128,128]{6,5,4,3,2,0,1:T(8,128)(2,1)}), bf16[1,64,1,4,2,128,128]{6,5,4,3,2,0,1:T(8,128)(2,1)}) %all-gather.11.cloned.1.call-update) | async-done | bytes 16777232 | tf_op jit(solution)/shard_map/all_gather | solution.py:54
  117.7 22.7 %copy.62 = bf16[1,64,1,4,2,128,128]{5,6,4,3,1,2,0:T(8,128)(2,1)} copy(bf16[1,64,1,4,2,128,128]{6,5,4,3,2,0,1:T(8,128)(2,1)} %all-gather.11.cloned.1.call-done) | data formatting | bytes 33554432 | tf_op jit(solution)/shard_map/all_gather | solution.py:54
  140.5 128.2 %all-gather.13.cloned.1.call-done = bf16[1,64,2,2,128,128]{5,4,3,2,0,1:T(8,128)(2,1)} async-done(((bf16[1,16,2,2,128,128]{5,4,3,2,0,1:T(8,128)(2,1)}), bf16[1,64,2,2,128,128]{5,4,3,2,0,1:T(8,128)(2,1)}) %all-gather.13.cloned.1.call-update) | async-done | bytes 8388624 | tf_op jit(solution)/shard_map/all_gather | solution.py:63
  268.7 18.5 %convolution_bitcast_fusion.3 = f32[16,2,4,2,2,128,128]{5,6,3,1,4,2,0:T(8,128)} fusion(bf16[1,64,4,2,128,128]{4,5,3,2,1,0:T(8,128)(2,1)} %bitcast.137, bf16[1,64,2,2,128,128]{5,4,3,2,1,0:T(8,128)(2,1)} %bitcast.149), kind=kOutput, calls=%fused_computation.11 | convolution fusion | flops 2147483648 | bytes 39845888 | tf_op jit(solution)/shard_map/kmcij,kndjl->kmncdil/dot_general | solution.py:19
  287.2 18.5 %convolution_bitcast_fusion.2 = f32[16,2,4,2,2,128,128]{5,6,3,1,4,2,0:T(8,128)} fusion(bf16[1,64,4,2,128,128]{4,5,3,2,1,0:T(8,128)(2,1)} %bitcast.138, bf16[1,64,2,2,128,128]{5,4,3,2,1,0:T(8,128)(2,1)} %bitcast.150), kind=kOutput, calls=%fused_computation.10 | convolution fusion | flops 2147483648 | bytes 39845888 | tf_op jit(solution)/shard_map/kmcij,kndjl->kmncdil/dot_general | solution.py:19
  305.6 18.7 %convolution_bitcast_fusion.1 = f32[16,2,4,2,2,128,128]{5,6,3,1,4,2,0:T(8,128)} fusion(bf16[1,64,4,2,128,128]{4,5,3,2,1,0:T(8,128)(2,1)} %bitcast.139, bf16[1,64,2,2,128,128]{5,4,3,2,1,0:T(8,128)(2,1)} %bitcast.151), kind=kOutput, calls=%fused_computation.9 | convolution fusion | flops 2147483648 | bytes 39845888 | tf_op jit(solution)/shard_map/kmcij,kndjl->kmncdil/dot_general | solution.py:19
  324.3 18.5 %convolution_bitcast_fusion = f32[16,2,4,2,2,128,128]{5,6,3,1,4,2,0:T(8,128)} fusion(bf16[1,64,4,2,128,128]{4,5,3,2,1,0:T(8,128)(2,1)} %bitcast.140, bf16[1,64,2,2,128,128]{5,4,3,2,1,0:T(8,128)(2,1)} %bitcast.152), kind=kOutput, calls=%fused_computation.8 | convolution fusion | flops 2147483648 | bytes 39845888 | tf_op jit(solution)/shard_map/kmcij,kndjl->kmncdil/dot_general | solution.py:19
  342.7 19.3 %slice_subtract_fusion.3 = (f32[16,2,4,1,1,128,128]{5,6,3,1,4,2,0:T(8,128)}, f32[16,2,4,1,1,128,128]{5,6,3,1,4,2,0:T(8,128)}) fusion(f32[16,2,4,2,2,128,128]{5,6,3,1,4,2,0:T(8,128)} %convolution_bitcast_fusion.3), kind=kLoop, calls=%fused_computation.19 | loop fusion | flops 4194304 | bytes 50331648 | tf_op jit(solution)/shard_map/sub | solution.py:22
  362.1 9.3 %copy.65 = f32[16,2,4,1,1,128,128]{6,5,2,1,0,4,3:T(8,128)} copy(f32[16,2,4,1,1,128,128]{5,6,3,1,4,2,0:T(8,128)} %get-tuple-element.11) | data formatting | bytes 16777216 | tf_op jit(solution)/shard_map/sub | solution.py:22
  371.4 9.2 %copy.66 = f32[16,2,4,1,1,128,128]{6,5,2,1,0,4,3:T(8,128)} copy(f32[16,2,4,1,1,128,128]{5,6,3,1,4,2,0:T(8,128)} %get-tuple-element.12) | data formatting | bytes 16777216 | tf_op jit(solution)/shard_map/add | solution.py:23
  380.6 6.8 maximum_multiply_fusion
  387.4 6.0 copy.73
  393.4 19.4 %slice_subtract_fusion.2 = (f32[16,2,4,1,1,128,128]{5,6,3,1,4,2,0:T(8,128)}, f32[16,2,4,1,1,128,128]{5,6,3,1,4,2,0:T(8,128)}) fusion(f32[16,2,4,2,2,128,128]{5,6,3,1,4,2,0:T(8,128)} %convolution_bitcast_fusion.2), kind=kLoop, calls=%fused_computation.17 | loop fusion | flops 4194304 | bytes 50331648 | tf_op jit(solution)/shard_map/sub | solution.py:22
  412.8 9.5 %copy.79 = f32[16,2,4,1,1,128,128]{6,5,2,1,0,4,3:T(8,128)} copy(f32[16,2,4,1,1,128,128]{5,6,3,1,4,2,0:T(8,128)} %get-tuple-element.9) | data formatting | bytes 16777216 | tf_op jit(solution)/shard_map/sub | solution.py:22
  422.3 9.2 %copy.80 = f32[16,2,4,1,1,128,128]{6,5,2,1,0,4,3:T(8,128)} copy(f32[16,2,4,1,1,128,128]{5,6,3,1,4,2,0:T(8,128)} %get-tuple-element.10) | data formatting | bytes 16777216 | tf_op jit(solution)/shard_map/add | solution.py:23
  431.5 6.8 maximum_multiply_fusion.1
  438.3 6.1 copy.85
  444.4 19.3 %slice_subtract_fusion.1 = (f32[16,2,4,1,1,128,128]{5,6,3,1,4,2,0:T(8,128)}, f32[16,2,4,1,1,128,128]{5,6,3,1,4,2,0:T(8,128)}) fusion(f32[16,2,4,2,2,128,128]{5,6,3,1,4,2,0:T(8,128)} %convolution_bitcast_fusion.1), kind=kLoop, calls=%fused_computation.15 | loop fusion | flops 4194304 | bytes 50331648 | tf_op jit(solution)/shard_map/sub | solution.py:22
  463.7 9.2 %copy.91 = f32[16,2,4,1,1,128,128]{6,5,2,1,0,4,3:T(8,128)} copy(f32[16,2,4,1,1,128,128]{5,6,3,1,4,2,0:T(8,128)} %get-tuple-element.7) | data formatting | bytes 16777216 | tf_op jit(solution)/shard_map/sub | solution.py:22
  473.0 9.2 %copy.92 = f32[16,2,4,1,1,128,128]{6,5,2,1,0,4,3:T(8,128)} copy(f32[16,2,4,1,1,128,128]{5,6,3,1,4,2,0:T(8,128)} %get-tuple-element.8) | data formatting | bytes 16777216 | tf_op jit(solution)/shard_map/add | solution.py:23
  482.2 6.8 maximum_multiply_fusion.2
  489.0 6.1 copy.97
  495.1 19.3 %slice_subtract_fusion = (f32[16,2,4,1,1,128,128]{5,6,3,1,4,2,0:T(8,128)}, f32[16,2,4,1,1,128,128]{5,6,3,1,4,2,0:T(8,128)}) fusion(f32[16,2,4,2,2,128,128]{5,6,3,1,4,2,0:T(8,128)} %convolution_bitcast_fusion), kind=kLoop, calls=%fused_computation.13 | loop fusion | flops 4194304 | bytes 50331648 | tf_op jit(solution)/shard_map/sub | solution.py:22
  514.4 9.2 %copy.103 = f32[16,2,4,1,1,128,128]{6,5,2,1,0,4,3:T(8,128)} copy(f32[16,2,4,1,1,128,128]{5,6,3,1,4,2,0:T(8,128)} %get-tuple-element.5) | data formatting | bytes 16777216 | tf_op jit(solution)/shard_map/sub | solution.py:22
  523.6 9.2 %copy.104 = f32[16,2,4,1,1,128,128]{6,5,2,1,0,4,3:T(8,128)} copy(f32[16,2,4,1,1,128,128]{5,6,3,1,4,2,0:T(8,128)} %get-tuple-element.6) | data formatting | bytes 16777216 | tf_op jit(solution)/shard_map/add | solution.py:23
  532.9 6.8 maximum_multiply_fusion.3
  539.7 6.0 copy.109
  545.7 7.9 %broadcast_in_dim.26 = f32[8,16,2,128,128]{4,3,2,1,0:T(8,128)} broadcast(f32[]{:T(128)} %constant.0.clone.1), dimensions={} | broadcast | bytes 16777220 | tf_op jit(solution)/shard_map/broadcast_in_dim | solution.py:52
  553.6 39.5 %scatter_fusion = f32[8,16,2,128,128]{4,3,2,1,0:T(8,128)} fusion(f32[8,16,2,128,128]{4,3,2,1,0:T(8,128)} %broadcast_in_dim.26, s32[128]{0:T(128)S(1)} %copy-done.3, f32[128,2,128,128]{3,2,1,0:T(8,128)} %copy.73), kind=kCustom, calls=%fused_computation | custom fusion | flops 4194304 | bytes 50332672 | tf_op jit(solution)/shard_map/scatter-add | solution.py:30
  593.0 39.8 %scatter_fusion.1 = f32[8,16,2,128,128]{4,3,2,1,0:T(8,128)} fusion(f32[8,16,2,128,128]{4,3,2,1,0:T(8,128)} %scatter_fusion, s32[128]{0:T(128)S(1)} %copy-done.2, f32[128,2,128,128]{3,2,1,0:T(8,128)} %copy.85), kind=kCustom, calls=%fused_computation.1 | custom fusion | flops 4194304 | bytes 50332672 | tf_op jit(solution)/shard_map/scatter-add | solution.py:30
  632.9 39.7 %scatter_fusion.2 = f32[8,16,2,128,128]{4,3,2,1,0:T(8,128)} fusion(f32[8,16,2,128,128]{4,3,2,1,0:T(8,128)} %scatter_fusion.1, s32[128]{0:T(128)S(1)} %copy-done.1, f32[128,2,128,128]{3,2,1,0:T(8,128)} %copy.97), kind=kCustom, calls=%fused_computation.2 | custom fusion | flops 4194304 | bytes 50332672 | tf_op jit(solution)/shard_map/scatter-add | solution.py:30
  672.5 39.7 %scatter_fusion.3 = f32[8,16,2,128,128]{4,3,2,1,0:T(8,128)} fusion(f32[8,16,2,128,128]{4,3,2,1,0:T(8,128)} %scatter_fusion.2, s32[128]{0:T(128)S(1)} %copy-done, f32[128,2,128,128]{3,2,1,0:T(8,128)} %copy.109), kind=kCustom, calls=%fused_computation.3 | custom fusion | flops 4194304 | bytes 50332672 | tf_op jit(solution)/shard_map/scatter-add | solution.py:30
  712.3 9.2 %convert_element_type.55 = bf16[8,16,2,128,128]{4,3,2,1,0:T(8,128)(2,1)} convert(f32[8,16,2,128,128]{4,3,2,1,0:T(8,128)} %scatter_fusion.3) | non-fusion elementwise | flops 4194304 | bytes 25165824 | tf_op jit(solution)/shard_map/convert_element_type | solution.py:77
  (55 shorter events, 6.7 us)
Async XLA Ops:
  6.5 111.2 %all-gather.11.cloned.1.call-start = ((), (), s32[]{:S(2)}) async-start(), calls=%async_computation | async-start | bytes 20971520 | tf_op jit(solution)/shard_map/all_gather | solution.py:54
  7.3 261.4 %all-gather.13.cloned.1.call-start = ((), (), s32[]{:S(2)}) async-start(), calls=%async_computation.1 | async-start | bytes 10485760 | tf_op jit(solution)/shard_map/all_gather | solution.py:63
  473.0 9.2 %copy-start.4 = (f32[128]{0:T(128)S(1)}, f32[128]{0:T(128)}, u32[]{:S(2)}) copy-start(f32[128]{0:T(128)} %reshape.718) | copy-start | bytes 1540
  523.6 9.2 %copy-start.5 = (f32[128]{0:T(128)S(1)}, f32[128]{0:T(128)}, u32[]{:S(2)}) copy-start(f32[128]{0:T(128)} %reshape.719) | copy-start | bytes 1540
  545.7 7.9 %copy-start.3 = (s32[128]{0:T(128)S(1)}, s32[128]{0:T(128)}, u32[]{:S(2)}) copy-start(s32[128]{0:T(128)} %fusion.4) | copy-start | bytes 1540
  553.6 39.5 %copy-start.2 = (s32[128]{0:T(128)S(1)}, s32[128]{0:T(128)}, u32[]{:S(2)}) copy-start(s32[128]{0:T(128)} %fusion.5) | copy-start | bytes 1540
  593.0 39.8 %copy-start.1 = (s32[128]{0:T(128)S(1)}, s32[128]{0:T(128)}, u32[]{:S(2)}) copy-start(s32[128]{0:T(128)} %fusion.6) | copy-start | bytes 1540
  632.9 39.7 %copy-start = (s32[128]{0:T(128)S(1)}, s32[128]{0:T(128)}, u32[]{:S(2)}) copy-start(s32[128]{0:T(128)} %fusion.7) | copy-start | bytes 1540
Sparse Core Ops, SparseCore 0:
  8.9 108.8 all-gather.10
  119.3 149.3 all-gather.12
where the time goes:
time: 733 us; the launch traced here: 729 us
  other arithmetic  275 us (38%)
  waiting for transfers between devices  173 us (24%)
  local copies, waits for them, and re-layouts  139 us (19%)
  matrix products  74 us (10%)
  blocking collectives  51.6 us (7%)
  between operations  15 us (2%)
    scatter-add x4, other arithmetic, pair_products(): total.at[row_index, col_index].add(product.reshape(-1, 2, width, width))  159 us
    all_gather x1, waiting for transfers between devices, body(): lax.all_gather(left_pack[0], 'col', axis=0, tiled=True)  128 us
    sub x4, other arithmetic, pair_products(): real_part = terms[:, :, :, 0, 0] - terms[:, :, :, 1, 1]  77.3 us
    dot_general x4, matrix products, pair_products(): jnp.einsum('kmcij,kndjl->kmncdil', left_blocks, right_blocks, preferred_e...  74 us
    all_gather x1, waiting for transfers between devices, body(): lax.all_gather(right_pack[0], 'row', axis=1, tiled=True)  43.8 us
    sub x4, local copies, waits for them, and re-layouts, pair_products(): real_part = terms[:, :, :, 0, 0] - terms[:, :, :, 1, 1]  37.2 us
    add x4, local copies, waits for them, and re-layouts, pair_products(): imag_part = terms[:, :, :, 0, 1] + terms[:, :, :, 1, 0]  37 us
    mul x4, other arithmetic, pair_products(): jnp.stack([real_part, imag_part], axis=3)  27.1 us
  transfers between devices with their start and end apart: 2, of which 2 were waited for; matrix products, arithmetic and copies ran while one was open for 5% of the time, Pallas kernels for 0%

commit v1 on v0

--- a/solution.py
+++ b/solution.py
@@ -5,6 +5,16 @@
 
 GR = 8
 LEVEL_CUT = 7
+
+
+def ring_gather(x, axis, dim):
+    ways, here, hop = (lax.axis_size(axis), lax.axis_index(axis), x.shape[dim])
+    shape = [n * ways if d == dim else n for d, n in enumerate(x.shape)]
+    full = lax.dynamic_update_slice_in_dim(jnp.zeros(shape, x.dtype), x, here * hop, axis=dim)
+    for far in range(1, ways):
+        x = lax.ppermute(x, axis, [(d, (d + 1) % ways) for d in range(ways)])
+        full = lax.dynamic_update_slice_in_dim(full, x, (here - far) % ways * hop, axis=dim)
+    return full
 
 
 def pair_products(left_pack, right_pack, total):
@@ -60,7 +70,7 @@
     flat = jax.tree.map(lambda member: member.reshape((merged,) + member.shape[2:]), whole)
     carry = total
     piece = (
-        lax.all_gather(left_pack[0], "col", axis=0, tiled=True),
+        ring_gather(left_pack[0], "col", 0),
         lax.all_gather(left_pack[1], "col", axis=0, tiled=True),
         lax.all_gather(left_pack[2], "col", axis=0, tiled=True),
         lax.all_gather(left_pack[3], "col", axis=0, tiled=True),

time: 733 us -> 593 us (0.81)
  local copies, waits for them, and re-layouts: 139 us -> 37 us
  waiting for transfers between devices: 173 us -> 75 us
  blocking collectives: 51.6 us -> 88.1 us
  other arithmetic: 275 us -> 291 us
    all_gather x1 -> x0, waiting for transfers between devices: 128 us -> none  [body(): lax.all_gather(left_pack[0], 'col', axis=0, tiled=True)]
    ppermute x0 -> x3, waiting for transfers between devices: none -> 74.3 us  [ring_gather(): x = lax.ppermute(x, axis, [(d, (d + 1) % ways) for d in range(ways)])]
    all_gather x1, waiting for transfers between devices: 43.8 us -> 0.01 us  [body(): lax.all_gather(right_pack[0], 'row', axis=1, tiled=True)]
    all_gather x1, blocking collectives: 11.6 us -> 49.7 us  [body(): lax.all_gather(left_pack[3], 'col', axis=0, tiled=True)]
    sub x4 -> x0, local copies, waits for them, and re-layouts: 37.2 us -> none  [pair_products(): real_part = terms[:, :, :, 0, 0] - terms[:, :, :, 1, 1]]
    add x4 -> x0, local copies, waits for them, and re-layouts: 37 us -> none  [pair_products(): imag_part = terms[:, :, :, 0, 1] + terms[:, :, :, 1, 0]]
    mul x4 -> x0, local copies, waits for them, and re-layouts: 24.3 us -> none  [pair_products(): jnp.stack([real_part, imag_part], axis=3)]
    all_gather x1 -> x0, local copies, waits for them, and re-layouts: 22.7 us -> none  [body(): lax.all_gather(right_pack[0], 'row', axis=1, tiled=True)]
  transfers between devices with their start and end apart: 2 -> 4, of which waited for: 2 -> 2; matrix products, arithmetic and copies ran while one was open for 5% -> 5% of each run, Pallas kernels for 0% -> 0%
where the time goes in v1:
time: 593 us; the launch traced here: 582 us
  other arithmetic  291 us (49%)
  blocking collectives  88.1 us (15%)
  waiting for transfers between devices  75 us (13%)
  matrix products  74.1 us (12%)
  local copies, waits for them, and re-layouts  37 us (6%)
  between operations  15.2 us (3%)
    scatter-add x4, other arithmetic, pair_products(): total.at[row_index, col_index].add(product.reshape(-1, 2, width, width))  158 us
    sub x4, other arithmetic, pair_products(): real_part = terms[:, :, :, 0, 0] - terms[:, :, :, 1, 1]  77 us
    ppermute x3, waiting for transfers between devices, ring_gather(): x = lax.ppermute(x, axis, [(d, (d + 1) % ways) for d in range(ways)])  74.3 us
    dot_general x4, matrix products, pair_products(): jnp.einsum('kmcij,kndjl->kmncdil', left_blocks, right_blocks, preferred_e...  74.1 us
    all_gather x1, blocking collectives, body(): lax.all_gather(left_pack[3], 'col', axis=0, tiled=True)  49.7 us
    mul x4, other arithmetic, pair_products(): jnp.stack([real_part, imag_part], axis=3)  44 us
    unnamed x2, blocking collectives  14.4 us
  transfers between devices with their start and end apart: 4, of which 2 were waited for; matrix products, arithmetic and copies ran while one was open for 5% of the time, Pallas kernels for 0%

profile of v1, /device:TPU:1, one launch (start us, length us, event | category | flops | bytes accessed | tf_op | source)
XLA Modules:
  0.0 582.2 jit_solution(12254186339281514638)
XLA Ops:
  6.5 0.7 all-gather.9.cloned.1.call-update
  7.3 2.2 collective-permute-start
  9.4 1.2 dynamic-slice.1
  10.7 1.3 dynamic-slice
  13.3 0.8 bitcast_dynamic-update-slice_fusion
  14.1 43.0 %collective-permute-done = bf16[16,2,2,128,128]{4,3,2,1,0:T(8,128)(2,1)} collective-permute-done((bf16[16,2,2,128,128]{4,3,2,1,0:T(8,128)(2,1)}, bf16[16,2,2,128,128]{4,3,2,1,0:T(8,128)(2,1)}, u32[]{:S(2)}, u32[]{:S(2)}) %collective-permute-start) | collective-permute-done | bytes 2097184 | tf_op jit(solution)/shard_map/ppermute | solution.py:15
  57.1 0.7 bitcast_dynamic-update-slice_fusion.1
  57.8 0.8 copy.68
  58.6 0.8 copy.71
  59.4 0.8 copy.59
  60.1 0.8 copy.62
  60.9 49.7 %all-gather.5 = s32[1,64,2]{2,0,1:T(1,128)S(1)} all-gather(s32[1,16,2]{2,0,1:T(1,128)S(1)} %copy.68), channel_id=7, replica_groups=mesh['kpt'=2,'row'=4,'col'=4] {'col'}, dimensions={1}, use_global_device_ids=true | all-gather | bytes 640 | tf_op jit(solution)/shard_map/all_gather | solution.py:76
  110.5 10.5 %all-gather = s32[1,64,2]{2,0,1:T(1,128)S(1)} all-gather(s32[1,16,2]{2,0,1:T(1,128)S(1)} %copy.59), channel_id=2, replica_groups=mesh['kpt'=2,'row'=4,'col'=4] {'col'}, dimensions={1}, use_global_device_ids=true | all-gather | bytes 640 | tf_op jit(solution)/shard_map/all_gather | solution.py:74
  121.0 10.0 %all-reduce.1 = s32[64]{0:T(128)S(1)} all-reduce(s32[64]{0:T(128)S(1)} %bitcast_dynamic-update-slice_fusion), channel_id=6, replica_groups=mesh['kpt'=2,'row'=4,'col'=4] {'row'}, use_global_device_ids=true, to_apply=%add.1 | all-reduce | flops 64 | bytes 512
  131.0 4.4 all-reduce
  135.4 8.4 %all-gather.6 = s32[1,64,1,4]{3,2,0,1:T(1,128)S(1)} all-gather(s32[1,16,1,4]{3,2,0,1:T(1,128)S(1)} %copy.71), channel_id=8, replica_groups=mesh['kpt'=2,'row'=4,'col'=4] {'row'}, dimensions={1}, use_global_device_ids=true | all-gather | bytes 1280 | tf_op jit(solution)/shard_map/all_gather | solution.py:67
  143.8 5.2 all-gather.1
  150.0 0.1 reshape.708
  150.3 0.1 reshape.710
  150.8 0.6 reshape.718
  152.2 0.7 reshape.719
  152.9 0.5 fusion.4
  153.4 0.6 fusion.6
  154.0 5.5 broadcast_in_dim.32
  159.6 1.5 constant_dynamic-update-slice_fusion.3
  161.0 3.2 constant_dynamic-update-slice_fusion.2
  164.2 3.2 constant_dynamic-update-slice_fusion.1
  167.3 31.3 %collective-permute-done.2 = bf16[16,2,2,128,128]{4,3,2,1,0:T(8,128)(2,1)} collective-permute-done((bf16[16,2,2,128,128]{4,3,2,1,0:T(8,128)(2,1)}, bf16[16,2,2,128,128]{4,3,2,1,0:T(8,128)(2,1)}, u32[]{:S(2)}, u32[]{:S(2)}) %collective-permute-start.2) | collective-permute-done | bytes 2097184 | tf_op jit(solution)/shard_map/ppermute | solution.py:15
  198.6 3.2 constant_dynamic-update-slice_fusion
  201.8 18.4 %convolution_bitcast_fusion.2 = f32[16,2,4,2,2,128,128]{6,5,4,2,3,1,0:T(8,128)} fusion(bf16[1,64,4,2,128,128]{5,4,3,2,1,0:T(8,128)(2,1)} %bitcast.150, bf16[64,2,2,128,128]{4,3,2,1,0:T(8,128)(2,1)} %constant_dynamic-update-slice_fusion), kind=kOutput, calls=%fused_computation.10 | convolution fusion | flops 2147483648 | bytes 39845888 | tf_op jit(solution)/shard_map/kmcij,kndjl->kmncdil/dot_general | solution.py:29
  220.2 18.9 %convolution_bitcast_fusion.3 = f32[16,2,4,2,2,128,128]{6,5,4,2,3,1,0:T(8,128)} fusion(bf16[1,64,4,2,128,128]{5,4,3,2,1,0:T(8,128)(2,1)} %bitcast.151, bf16[64,2,2,128,128]{4,3,2,1,0:T(8,128)(2,1)} %constant_dynamic-update-slice_fusion), kind=kOutput, calls=%fused_computation.11 | convolution fusion | flops 2147483648 | bytes 39845888 | tf_op jit(solution)/shard_map/kmcij,kndjl->kmncdil/dot_general | solution.py:29
  239.1 18.4 %convolution_bitcast_fusion.1 = f32[16,2,4,2,2,128,128]{6,5,4,2,3,1,0:T(8,128)} fusion(bf16[1,64,4,2,128,128]{5,4,3,2,1,0:T(8,128)(2,1)} %bitcast.152, bf16[64,2,2,128,128]{4,3,2,1,0:T(8,128)(2,1)} %constant_dynamic-update-slice_fusion), kind=kOutput, calls=%fused_computation.9 | convolution fusion | flops 2147483648 | bytes 39845888 | tf_op jit(solution)/shard_map/kmcij,kndjl->kmncdil/dot_general | solution.py:29
  257.5 18.4 %convolution_bitcast_fusion = f32[16,2,4,2,2,128,128]{6,5,4,2,3,1,0:T(8,128)} fusion(bf16[1,64,4,2,128,128]{5,4,3,2,1,0:T(8,128)(2,1)} %bitcast.153, bf16[64,2,2,128,128]{4,3,2,1,0:T(8,128)(2,1)} %constant_dynamic-update-slice_fusion), kind=kOutput, calls=%fused_computation.8 | convolution fusion | flops 2147483648 | bytes 39845888 | tf_op jit(solution)/shard_map/kmcij,kndjl->kmncdil/dot_general | solution.py:29
  275.9 19.3 %slice_subtract_fusion.2 = (f32[16,2,4,1,1,128,128]{6,5,4,2,3,1,0:T(8,128)}, f32[16,2,4,1,1,128,128]{6,5,4,2,3,1,0:T(8,128)}) fusion(f32[16,2,4,2,2,128,128]{6,5,4,2,3,1,0:T(8,128)} %convolution_bitcast_fusion.2), kind=kLoop, calls=%fused_computation.17 | loop fusion | flops 4194304 | bytes 50331648 | tf_op jit(solution)/shard_map/sub | solution.py:32
  295.2 19.4 %slice_subtract_fusion.3 = (f32[16,2,4,1,1,128,128]{6,5,4,2,3,1,0:T(8,128)}, f32[16,2,4,1,1,128,128]{6,5,4,2,3,1,0:T(8,128)}) fusion(f32[16,2,4,2,2,128,128]{6,5,4,2,3,1,0:T(8,128)} %convolution_bitcast_fusion.3), kind=kLoop, calls=%fused_computation.19 | loop fusion | flops 4194304 | bytes 50331648 | tf_op jit(solution)/shard_map/sub | solution.py:32
  314.5 19.2 %slice_subtract_fusion.1 = (f32[16,2,4,1,1,128,128]{6,5,4,2,3,1,0:T(8,128)}, f32[16,2,4,1,1,128,128]{6,5,4,2,3,1,0:T(8,128)}) fusion(f32[16,2,4,2,2,128,128]{6,5,4,2,3,1,0:T(8,128)} %convolution_bitcast_fusion.1), kind=kLoop, calls=%fused_computation.15 | loop fusion | flops 4194304 | bytes 50331648 | tf_op jit(solution)/shard_map/sub | solution.py:32
  333.7 19.1 %slice_subtract_fusion = (f32[16,2,4,1,1,128,128]{6,5,4,2,3,1,0:T(8,128)}, f32[16,2,4,1,1,128,128]{6,5,4,2,3,1,0:T(8,128)}) fusion(f32[16,2,4,2,2,128,128]{6,5,4,2,3,1,0:T(8,128)} %convolution_bitcast_fusion), kind=kLoop, calls=%fused_computation.13 | loop fusion | flops 4194304 | bytes 50331648 | tf_op jit(solution)/shard_map/sub | solution.py:32
  352.9 13.8 %maximum_multiply_fusion.1 = f32[128,2,128,128]{3,2,1,0:T(8,128)} fusion(f32[128,1,128,128]{3,2,1,0:T(8,128)} %bitcast.149, f32[128,1,128,128]{3,2,1,0:T(8,128)} %bitcast.148, f32[128]{0:T(128)S(1)} %reshape.717), kind=kLoop, calls=%fused_computation.5 | loop fusion | flops 8388608 | bytes 33554944 | tf_op jit(solution)/shard_map/mul | solution.py:34
  366.7 2.6 copy-done.1
  369.4 6.3 %maximum_multiply_fusion = f32[128,2,128,128]{3,2,1,0:T(8,128)} fusion(f32[128,1,128,128]{3,2,1,0:T(8,128)S(1)} %bitcast.147, f32[128,1,128,128]{3,2,1,0:T(8,128)S(1)} %bitcast.146, f32[128]{0:T(128)S(1)} %reshape.716), kind=kLoop, calls=%fused_computation.4 | loop fusion | flops 8388608 | bytes 33554944 | tf_op jit(solution)/shard_map/mul | solution.py:34
  375.6 7.9 %broadcast_in_dim.28 = f32[8,16,2,128,128]{4,3,2,1,0:T(8,128)} broadcast(f32[]{:T(128)} %constant.36.clone.1), dimensions={} | broadcast | bytes 16777220 | tf_op jit(solution)/shard_map/broadcast_in_dim | solution.py:62
  383.5 39.5 %scatter_fusion = f32[8,16,2,128,128]{4,3,2,1,0:T(8,128)} fusion(f32[8,16,2,128,128]{4,3,2,1,0:T(8,128)} %broadcast_in_dim.28, s32[128]{0:T(128)S(1)} %get-tuple-element.37, f32[128,2,128,128]{3,2,1,0:T(8,128)} %maximum_multiply_fusion), kind=kCustom, calls=%fused_computation | custom fusion | flops 4194304 | bytes 50332672 | tf_op jit(solution)/shard_map/scatter-add | solution.py:40
  423.0 39.7 %scatter_fusion.1 = f32[8,16,2,128,128]{4,3,2,1,0:T(8,128)} fusion(f32[8,16,2,128,128]{4,3,2,1,0:T(8,128)} %scatter_fusion, s32[128]{0:T(128)S(1)} %copy-done.4, f32[128,2,128,128]{3,2,1,0:T(8,128)} %maximum_multiply_fusion.1), kind=kCustom, calls=%fused_computation.1 | custom fusion | flops 4194304 | bytes 50332672 | tf_op jit(solution)/shard_map/scatter-add | solution.py:40
  462.7 12.0 %maximum_multiply_fusion.2 = f32[128,2,128,128]{3,2,1,0:T(8,128)} fusion(f32[128,1,128,128]{3,2,1,0:T(8,128)} %bitcast.145, f32[128,1,128,128]{3,2,1,0:T(8,128)} %bitcast.144, f32[128]{0:T(128)S(1)} %copy-done.6), kind=kLoop, calls=%fused_computation.6 | loop fusion | flops 8388608 | bytes 33554944 | tf_op jit(solution)/shard_map/mul | solution.py:34
  474.7 39.6 %scatter_fusion.2 = f32[8,16,2,128,128]{4,3,2,1,0:T(8,128)} fusion(f32[8,16,2,128,128]{4,3,2,1,0:T(8,128)} %scatter_fusion.1, s32[128]{0:T(128)S(1)} %copy-done.3, f32[128,2,128,128]{3,2,1,0:T(8,128)} %maximum_multiply_fusion.2), kind=kCustom, calls=%fused_computation.2 | custom fusion | flops 4194304 | bytes 50332672 | tf_op jit(solution)/shard_map/scatter-add | solution.py:40
  514.3 12.0 %maximum_multiply_fusion.3 = f32[128,2,128,128]{3,2,1,0:T(8,128)} fusion(f32[128,1,128,128]{3,2,1,0:T(8,128)} %bitcast.143, f32[128,1,128,128]{3,2,1,0:T(8,128)} %bitcast.142, f32[128]{0:T(128)S(1)} %copy-done.7), kind=kLoop, calls=%fused_computation.7 | loop fusion | flops 8388608 | bytes 33554944 | tf_op jit(solution)/shard_map/mul | solution.py:34
  526.3 39.6 %scatter_fusion.3 = f32[8,16,2,128,128]{4,3,2,1,0:T(8,128)} fusion(f32[8,16,2,128,128]{4,3,2,1,0:T(8,128)} %scatter_fusion.2, s32[128]{0:T(128)S(1)} %copy-done.2, f32[128,2,128,128]{3,2,1,0:T(8,128)} %maximum_multiply_fusion.3), kind=kCustom, calls=%fused_computation.3 | custom fusion | flops 4194304 | bytes 50332672 | tf_op jit(solution)/shard_map/scatter-add | solution.py:40
  565.9 9.2 %convert_element_type.55 = bf16[8,16,2,128,128]{4,3,2,1,0:T(8,128)(2,1)} convert(f32[8,16,2,128,128]{4,3,2,1,0:T(8,128)} %scatter_fusion.3) | non-fusion elementwise | flops 4194304 | bytes 25165824 | tf_op jit(solution)/shard_map/convert_element_type | solution.py:87
  (52 shorter events, 2.2 us)
Async XLA Ops:
  6.5 153.0 %copy-start.5 = (bf16[1,16,2,2,128,128]{5,4,3,2,1,0:T(8,128)(2,1)S(1)}, bf16[1,16,2,2,128,128]{5,4,3,2,1,0:T(8,128)(2,1)}, u32[]{:S(2)}) copy-start(bf16[1,16,2,2,128,128]{5,4,3,2,1,0:T(8,128)(2,1)} %param.8) | copy-start | bytes 6291460
  6.5 195.2 %all-gather.9.cloned.1.call-start = ((), (), s32[]{:S(2)}) async-start(), calls=%async_computation | async-start | bytes 20971520 | tf_op jit(solution)/shard_map/all_gather | solution.py:64
  7.3 49.8 %collective-permute-start = (bf16[16,2,2,128,128]{4,3,2,1,0:T(8,128)(2,1)}, bf16[16,2,2,128,128]{4,3,2,1,0:T(8,128)(2,1)}, u32[]{:S(2)}, u32[]{:S(2)}) collective-permute-start(bf16[16,2,2,128,128]{4,3,2,1,0:T(8,128)(2,1)} %bitcast.155), channel_id=1, source_target_pairs={{0,1},{1,2},{2,3},{3,0},{4,5},{5,6},{6,7},{7,4},{8,9},{9,10},{10,1... | collective-permute-start | bytes 6291464 | tf_op jit(solution)/shard_map/ppermute | solution.py:15
  57.1 92.3 %collective-permute-start.1 = (bf16[16,2,2,128,128]{4,3,2,1,0:T(8,128)(2,1)}, bf16[16,2,2,128,128]{4,3,2,1,0:T(8,128)(2,1)}, u32[]{:S(2)}, u32[]{:S(2)}) collective-permute-start(bf16[16,2,2,128,128]{4,3,2,1,0:T(8,128)(2,1)} %collective-permute-done), channel_id=1, source_target_pairs={{0,1},{1,2},{2,3},{3,0},{4,5},{5,6},{6,7},{7,4},{8,9},{9,10},{10,1... | collective-permute-start | bytes 6291464 | tf_op jit(solution)/shard_map/ppermute | solution.py:15
  149.4 49.2 %collective-permute-start.2 = (bf16[16,2,2,128,128]{4,3,2,1,0:T(8,128)(2,1)}, bf16[16,2,2,128,128]{4,3,2,1,0:T(8,128)(2,1)}, u32[]{:S(2)}, u32[]{:S(2)}) collective-permute-start(bf16[16,2,2,128,128]{4,3,2,1,0:T(8,128)(2,1)} %collective-permute-done.1), channel_id=1, source_target_pairs={{0,1},{1,2},{2,3},{3,0},{4,5},{5,6},{6,7},{7,4},{8,9},{9,10},{10,1... | collective-permute-start | bytes 6291464 | tf_op jit(solution)/shard_map/ppermute | solution.py:15
  352.9 13.8 %copy-start = (f32[16,2,4,1,1,128,128]{6,5,4,2,3,1,0:T(8,128)S(1)}, f32[16,2,4,1,1,128,128]{6,5,4,2,3,1,0:T(8,128)}, u32[]{:S(2)}) copy-start(f32[16,2,4,1,1,128,128]{6,5,4,2,3,1,0:T(8,128)} %get-tuple-element.11) | copy-start | bytes 25165828
  352.9 16.5 %copy-start.1 = (f32[16,2,4,1,1,128,128]{6,5,4,2,3,1,0:T(8,128)S(1)}, f32[16,2,4,1,1,128,128]{6,5,4,2,3,1,0:T(8,128)}, u32[]{:S(2)}) copy-start(f32[16,2,4,1,1,128,128]{6,5,4,2,3,1,0:T(8,128)} %get-tuple-element.12) | copy-start | bytes 25165828
  383.5 39.5 %copy-start.4 = (s32[128]{0:T(128)S(1)}, s32[128]{0:T(128)}, u32[]{:S(2)}) copy-start(s32[128]{0:T(128)} %get-tuple-element.38) | copy-start | bytes 1540
  423.0 39.7 %copy-start.6 = (f32[128]{0:T(128)S(1)}, f32[128]{0:T(128)}, u32[]{:S(2)}) copy-start(f32[128]{0:T(128)} %reshape.718) | copy-start | bytes 1540
  462.7 12.0 %copy-start.3 = (s32[128]{0:T(128)S(1)}, s32[128]{0:T(128)}, u32[]{:S(2)}) copy-start(s32[128]{0:T(128)} %get-tuple-element.39) | copy-start | bytes 1540
  474.7 39.6 %copy-start.7 = (f32[128]{0:T(128)S(1)}, f32[128]{0:T(128)}, u32[]{:S(2)}) copy-start(f32[128]{0:T(128)} %reshape.719) | copy-start | bytes 1540
  514.3 12.0 %copy-start.2 = (s32[128]{0:T(128)S(1)}, s32[128]{0:T(128)}, u32[]{:S(2)}) copy-start(s32[128]{0:T(128)} %get-tuple-element.40) | copy-start | bytes 1540
Sparse Core Ops, SparseCore 0:
  8.9 108.3 all-gather.8
